TPU v7x, 512 devices: a whole 4x4x16 slice. The times are simulated.
512 devices in a mesh: segment: 16 (over z_hi, y, core), dp: 32 (over x, z_lo).
Axes of the slice: x: 4, y: 4, z: 16 (z_hi: 2, z_lo: 8; z = z_hi * 8 + z_lo), core: 2. Of those that a mesh axis runs over, the one named last changes fastest.
Arguments:
- token_ids: int32 [4096], P('dp'), may hold values from 0 to 152063, as said below
- table: bfloat16 [19008, 28672], P('segment', 'dp'), may hold values from -6 to 6
- out_grad: bfloat16 [4096, 3584], P('dp', 'segment'), may hold values from -6 to 6
Outputs:
- embedded: bfloat16 [4096, 3584], P('dp')
- table_grad: bfloat16 [19008, 28672], P('segment', 'dp')
Inputs may be any that keep to these rules, and one draw needn't show every extreme that they name: `token_ids`: in the 128 tokens of each data group, at most 16 ids lie in one segment's slice of 9504 rows with one residue modulo 8; in every data group some segment and residue has exactly 16.
All inputs are finite; a program needn't handle non-finite values.
Results may differ from a plain program's by a relative error of at most 0.001.
Values may be sent and summed in bfloat16 or wider, within the bound.
A program may use at most 64 MiB of HBM per device.

v0:
```python
import functools

import jax
import jax.numpy as jnp
from jax import lax
from jax.experimental import pallas as pl
from jax.experimental.pallas import tpu as pltpu
from jax.sharding import PartitionSpec as P

PACK = 8
BF = jnp.bfloat16
F32 = jnp.float32


def flip(index, bit):
    return index + bit - 2 * bit * ((index // bit) % 2)


def push(src, dst, send, recv, peer):
    copy = pltpu.make_async_remote_copy(
        src_ref=src,
        dst_ref=dst,
        send_sem=send,
        recv_sem=recv,
        device_id=peer,
        device_id_type=pl.DeviceIdType.MESH,
    )
    copy.start()
    return copy


def select(ids, first, lines, slot, cap):
    rows, tok = ids.shape
    local = ids - first
    owned = (local >= 0) & (local < lines * PACK) & (ids % PACK == slot)
    before = lax.broadcasted_iota(jnp.int32, (tok, tok), 0) < lax.broadcasted_iota(
        jnp.int32, (tok, tok), 1
    )
    rank = jnp.dot(
        jnp.where(owned, 1.0, 0.0).astype(BF),
        jnp.where(before, 1.0, 0.0).astype(BF),
        preferred_element_type=F32,
    )
    want = lax.broadcasted_iota(jnp.int32, (rows, tok), 0) % cap
    return owned & (rank.astype(jnp.int32) == want), local


def kernel(
    groups, segs, inside, chunk,
    ids_ref, table_ref, grad_ref,
    emb_ref, back_ref, hot_ref,
    ids_mine, ids_all, table, rows_out, rows_in, grads, back_out, part, halves, total,
    load_sem, ids_sem, raw_sem, grad_sem, fwd_sem, bwd_sem, seg_sem,
):
    dp = lax.axis_index("dp")
    seg = lax.axis_index("segment")
    lines, width = table.shape
    cap, tok = ids_mine.shape
    quarters = groups // PACK
    chunks = width // chunk
    half = tok // 2
    near = groups // 2
    base = (dp // near) * near
    mirror = (dp + near) % groups
    first = seg * lines * PACK
    core = seg % 2
    offsets = sorted(range(1, groups), key=lambda k: -min(k, groups - k))
    bits = [1 << b for b in range(segs.bit_length() - 1)]
    far = bits[::-1] if inside else []
    own = seg if inside else 0

    load_grad = pltpu.make_async_copy(grad_ref, grads.at[0, own], load_sem.at[0])
    load_grad.start()
    load = pltpu.make_async_copy(table_ref, table, load_sem.at[1])
    load.start()
    ids_mine[...] = jnp.broadcast_to(ids_ref[...], (cap, tok))
    barrier = pltpu.get_barrier_semaphore()
    for k in offsets:
        pl.semaphore_signal(
            barrier, inc=1, device_id={"dp": (dp + k) % groups},
            device_id_type=pl.DeviceIdType.MESH,
        )
    for b in bits:
        pl.semaphore_signal(
            barrier, inc=1, device_id={"segment": flip(seg, b)},
            device_id_type=pl.DeviceIdType.MESH,
        )
    load_grad.wait()
    pl.semaphore_wait(barrier, len(offsets) + len(bits))

    sent = []
    ids_copies = []
    for k in offsets:
        ids_copies.append(push(
            ids_mine, ids_all.at[dp], ids_sem.at[0, k], ids_sem.at[1, k],
            {"dp": (dp + k) % groups},
        ))
    raw = push(
        grads.at[0, own], grads.at[1, own], raw_sem.at[0], raw_sem.at[1], {"dp": mirror}
    )

    held = [[own], [own]]
    flying = [[], []]

    def gather_start(kind, level):
        for piece in held[kind]:
            n = len(sent_of[kind])
            copy = push(
                grads.at[kind, piece], grads.at[kind, piece],
                grad_sem.at[0, kind, n], grad_sem.at[1, kind, n],
                {"segment": flip(seg, far[level])},
            )
            sent_of[kind].append(copy)
            flying[kind].append(copy)

    def gather_wait(kind, level):
        for copy in flying[kind]:
            copy.wait_recv()
        flying[kind] = []
        held[kind] = held[kind] + [flip(piece, far[level]) for piece in held[kind]]

    sent_of = [[], []]
    if far:
        gather_start(0, 0)
    ids_all[dp] = ids_mine[...]

    slot_of = lax.broadcasted_iota(jnp.int32, (PACK * cap, tok), 0) // cap
    pick, _ = select(
        jnp.concatenate([ids_mine[...]] * PACK, axis=0), first, lines, slot_of, cap
    )
    scatter = jnp.where(pick, 1.0, 0.0).T.astype(BF)

    for copy in ids_copies:
        copy.wait_recv()
    named, local = select(
        ids_all[...].reshape(groups * cap, tok), first, lines, dp // quarters, cap
    )
    line = jnp.sum(
        jnp.where(named, (local // PACK + 1).astype(F32), 0.0), axis=1, keepdims=True
    ).astype(jnp.int32) - 1
    hot = jnp.where(
        lax.broadcasted_iota(jnp.int32, (groups * cap, lines), 1) == line, 1.0, 0.0
    ).astype(BF)
    hot_ref[...] = hot

    load.wait()
    fwd = []
    for f in range(chunks):
        cols = pl.ds(f * chunk, chunk)
        got = jnp.dot(hot_ref[...], table[:, cols], preferred_element_type=F32).astype(BF)
        rows_out[:, :, cols] = got.reshape(groups, cap, chunk)
        fwd.append([])
        for k in offsets:
            peer = (dp + k) % groups
            fwd[f].append(push(
                rows_out.at[peer, :, cols], rows_in.at[dp, :, cols],
                fwd_sem.at[0, k, f], fwd_sem.at[1, k, f], {"dp": peer},
            ))
    rows_in[dp] = rows_out[dp]

    slots_near = PACK // 2
    near_slot = base // quarters + lax.broadcasted_iota(
        jnp.int32, (slots_near * cap, tok), 0
    ) // cap
    depth = quarters * width
    piece_width = grads.shape[3]
    step = min(piece_width, width)
    bwd = []

    def dispatch(kind, group):
        pick, _ = select(
            jnp.concatenate([ids_all[group]] * slots_near, axis=0), first, lines, near_slot, cap
        )
        pick = jnp.where(pick, 1.0, 0.0).astype(BF)
        for at in range(0, depth, step):
            q, off = at // width, at % width
            inner = at % piece_width
            got = jnp.dot(
                pick, grads[kind, at // piece_width, :, inner:inner + step],
                preferred_element_type=F32,
            ).astype(BF)
            for r in range(slots_near):
                back_out[kind, r * quarters + q, :, off:off + step] = got[r * cap:(r + 1) * cap]
        for k in range(1, near):
            to = (dp - base + k) % near
            bwd.append(push(
                back_out.at[kind, to], back_ref.at[group],
                bwd_sem.at[0, kind, k], bwd_sem.at[1, kind, k], {"dp": base + to},
            ))
        back_ref[group] = back_out[kind, dp - base]

    for level in range(len(far)):
        if level > 0:
            gather_start(0, level)
        gather_wait(0, level)
    dispatch(0, dp)
    raw.wait_recv()
    for level in range(len(far)):
        gather_start(1, level)
        gather_wait(1, level)
    dispatch(1, mirror)

    tiles = [(f, q) for f in range(chunks) for q in range(quarters)]
    stages = len(bits) + 2
    moving = {}

    def seg_push(src, dst, level, n, bit):
        copy = push(
            src, dst, seg_sem.at[0, level, n], seg_sem.at[1, level, n],
            {"segment": flip(seg, bit)},
        )
        sent.append(copy)
        moving[n] = copy

    def advance(n, stage):
        f, q = tiles[n]
        at = q * width + f * chunk
        cols = pl.ds(at, chunk)
        if stage == 0:
            if q == 0:
                for copy in fwd[f]:
                    copy.wait_recv()
            got = jnp.concatenate(
                [rows_in[r * quarters + q, :, f * chunk:(f + 1) * chunk] for r in range(PACK)], axis=0
            )
            got = jnp.dot(scatter, got, preferred_element_type=F32).astype(BF)
            part[:, :, cols] = got.reshape(2, half, chunk)
            seg_push(part.at[1 - core, :, cols], halves.at[0, :, cols], 0, n, 1)
            return
        moving[n].wait_recv()
        if stage == stages - 1:
            return
        if stage == 1:
            total[0, :, cols] = part[core, :, cols] + halves[0, :, cols]
        else:
            total[stage - 1, :, cols] = total[stage - 2, :, cols] + halves[stage - 1, :, cols]
        src = total.at[stage - 1, :, cols]
        if stage < len(bits):
            seg_push(src, halves.at[stage, :, cols], stage, n, bits[stage])
        else:
            seg_push(src, emb_ref.at[core, :, cols], stage, n, 1)
            emb_ref[core, :, cols] = total[stage - 1, :, cols]

    for wave in range(len(tiles) + stages - 1):
        for stage in range(stages):
            if 0 <= wave - stage < len(tiles):
                advance(wave - stage, stage)

    for copy in bwd:
        copy.wait_recv()
    for copies in [sent, ids_copies, [raw], bwd] + sent_of + fwd:
        for copy in copies:
            copy.wait_send()


def body(token_ids, table, out_grad, groups, segs):
    lines, width = table.shape
    tok, piece = out_grad.shape
    depth = segs * piece
    cap = tok // PACK
    inside = piece % 128 == 0 and width % piece == 0
    if not inside:
        out_grad = lax.all_gather(out_grad, "segment", axis=1, tiled=True)
    pieces = segs if inside else 1
    chunk = width // 4 if width % 512 == 0 else width
    chunks = width // chunk
    levels = segs.bit_length() - 1
    vmem = pl.BlockSpec(memory_space=pltpu.VMEM)
    hbm = pl.BlockSpec(memory_space=pltpu.HBM)
    dma = pltpu.SemaphoreType.DMA
    emb, back, hot = pl.pallas_call(
        functools.partial(kernel, groups, segs, inside, chunk),
        out_shape=(
            jax.ShapeDtypeStruct((2, tok // 2, depth), BF),
            jax.ShapeDtypeStruct((groups, cap, width), BF),
            jax.ShapeDtypeStruct((groups * cap, lines), BF),
        ),
        in_specs=[vmem, hbm, hbm],
        out_specs=(vmem, vmem, vmem),
        scratch_shapes=[
            pltpu.VMEM((cap, tok), jnp.int32),
            pltpu.VMEM((groups, cap, tok), jnp.int32),
            pltpu.VMEM((lines, width), BF),
            pltpu.VMEM((groups, cap, width), BF),
            pltpu.VMEM((groups, cap, width), BF),
            pltpu.VMEM((2, pieces, tok, depth // pieces), BF),
            pltpu.VMEM((2, groups // 2, cap, width), BF),
            pltpu.VMEM((2, tok // 2, depth), BF),
            pltpu.VMEM((levels, tok // 2, depth), BF),
            pltpu.VMEM((levels, tok // 2, depth), BF),
            dma((2,)),
            dma((2, groups)),
            dma((2,)),
            dma((2, 2, segs)),
            dma((2, groups, chunks)),
            dma((2, 2, groups // 2)),
            dma((2, levels + 1, chunks * (groups // PACK))),
        ],
        compiler_params=pltpu.CompilerParams(
            collective_id=0, has_side_effects=True, vmem_limit_bytes=48 << 20
        ),
    )(token_ids[None, :], table, out_grad)
    grad = lax.dot_general(
        hot, back.reshape(groups * cap, width), (((0,), (0,)), ((), ())),
        preferred_element_type=F32,
    )
    return emb.reshape(tok, depth), grad.astype(BF)


def solution(mesh):
    placed = (P("dp"), P("segment", "dp"), P("dp", "segment"))
    return jax.shard_map(
        functools.partial(body, groups=mesh.shape["dp"], segs=mesh.shape["segment"]),
        mesh=mesh,
        in_specs=placed,
        out_specs=(P("dp", None), P("segment", "dp")),
        check_vma=False,
    )
```

profile of v0, /device:TPU:131, one launch (start us, length us, event | category | flops | bytes accessed | tf_op | source)
XLA Modules:
  0.0 216.5 jit_solution(484782656333758861)
XLA Ops:
  0.6 0.0 copy-start
  0.6 0.0 copy-start.1
  0.6 50.3 %all_gather.3 = bf16[128,3584]{0,1:T(8,128)(2,1)} all-gather(bf16[128,224]{0,1:T(8,128)(2,1)} %param.5), channel_id=1, replica_groups=mesh['segment'=16,'dp'=32] {'segment'}, dimensions={1}, use_global_device_ids=true | all-gather | bytes 974848 | tf_op jit(solution)/shard_map/all_gather | solution.py:263
  51.0 1.5 copy.6.grad_ref
  52.4 0.0 copy-done
  52.4 0.0 copy-done.1
  52.5 160.3 %shard_map.50 = (bf16[2,64,3584]{2,1,0:T(8,128)(2,1)S(1)}, bf16[32,16,896]{2,1,0:T(8,128)(2,1)S(1)}, bf16[512,1188]{1,0:T(8,128)(2,1)S(1)}) custom-call(s32[1,128]{1,0:T(1,128)S(1)} %bitcast.6, bf16[1188,896]{1,0:T(8,128)(2,1)S(1)} %copy-done, bf16[128,3584]{1,0:T(8,128)(2,1)S(1)} %copy.6.grad_ref), custom_call_target="tpu_custom_call" | custom-call | tf_op jit(solution)/shard_map/pallas_call | solution.py:271
  212.8 2.8 %convolution_convert_fusion = bf16[1188,896]{1,0:T(8,128)(2,1)} fusion(bf16[512,1188]{1,0:T(8,128)(2,1)S(1)} %get-tuple-element.6, bf16[512,896]{1,0:T(8,128)(2,1)S(1)} %bitcast.7), kind=kOutput, calls=%fused_computation | convolution fusion | flops 1091059200 | bytes 4262912 | tf_op jit(solution)/shard_map/dot_general | solution.py:303
  215.6 0.9 copy.8
Async XLA Ops:
  0.6 51.8 %copy-start = (bf16[1188,896]{1,0:T(8,128)(2,1)S(1)}, bf16[1188,896]{1,0:T(8,128)(2,1)}, u32[]{:S(2)}) copy-start(bf16[1188,896]{1,0:T(8,128)(2,1)} %table_ref.1) | copy-start | bytes 6386692
  0.6 51.8 %copy-start.1 = (s32[128]{0:T(128)S(1)}, s32[128]{0:T(128)}, u32[]{:S(2)}) copy-start(s32[128]{0:T(128)} %param.3) | copy-start | bytes 1540
where the time goes:
time: 217 us
  Pallas kernels  160 us (74%)
  blocking collectives  50.3 us (23%)
  matrix products  2.8 us (1%)
  local copies, waits for them, and re-layouts  2.38 us (1%)
    pallas_call x1, Pallas kernels, body(): pl.pallas_call(functools.partial(kernel, groups, segs, inside, chunk), ou...  160 us
    all_gather x1, blocking collectives, body(): out_grad = lax.all_gather(out_grad, 'segment', axis=1, tiled=True)  50.3 us

commit v1 on v0

v1 whole, which is shorter than its diff:
```python
import functools

import jax
import jax.numpy as jnp
from jax import lax
from jax.experimental import pallas as pl
from jax.experimental.pallas import tpu as pltpu
from jax.sharding import PartitionSpec as P

PACK = 8
BF = jnp.bfloat16
F32 = jnp.float32
MESH = pl.DeviceIdType.MESH

X, Y, Z, ZL = 4, 4, 16, 8
LANE = 128


def place(x, y, z, c):
    return {"segment": (z // ZL) * ZL + y * 2 + c, "dp": x * ZL + z % ZL}


def remote(src, dst, send, recv, peer):
    return pltpu.make_async_remote_copy(
        src_ref=src, dst_ref=dst, send_sem=send, recv_sem=recv,
        device_id=peer, device_id_type=MESH,
    )


def signal(sem, peer):
    pl.semaphore_signal(sem, inc=1, device_id=peer, device_id_type=MESH)


def ring(d, n):
    return min(d % n, n - d % n)


def choose(ids, first, span, slot, cap):
    rows, tok = ids.shape
    local = ids - first
    owned = (local >= 0) & (local < span) & ((ids & (PACK - 1)) == slot)
    before = lax.broadcasted_iota(jnp.int32, (tok, tok), 0) < lax.broadcasted_iota(
        jnp.int32, (tok, tok), 1
    )
    rank = jnp.dot(
        jnp.where(owned, 1.0, 0.0).astype(BF),
        jnp.where(before, 1.0, 0.0).astype(BF),
        preferred_element_type=F32,
    )
    want = lax.broadcasted_iota(jnp.int32, (rows, tok), 0) % cap
    return owned & (rank.astype(jnp.int32) == want), local


def kernel(
    ids_ref, table_ref, grad_ref,
    emb_ref, back_ref, hot_ref,
    ids_all, ids_wide, table, grad, raw_out, raw, rows_out, rows_in, pick, scatter,
    part, halves, sums, zin, back_out,
    load_sem, ids_sem, raw_sem, twin_sem, fwd_sem, half_sem, z_sem, bwd_sem, ag_sem, rel_sem,
):
    seg = lax.axis_index("segment")
    dp = lax.axis_index("dp")
    c = seg % 2
    y = (seg // 2) % Y
    zh = seg // ZL
    zl = dp % ZL
    z = zh * ZL + zl
    x = dp // ZL
    mine = x * Y + y
    k = 2 * y + c
    lines, width = table.shape
    tok = ids_ref.shape[1]
    feat = grad.shape[1]
    groups = X * ZL
    cap = rows_in.shape[3]
    blocks = width // LANE
    span = lines * PACK
    twin = place(x, y, z, 1 - c)

    ids_offs = sorted(
        [(dx, dz) for dx in range(X) for dz in range(-4, 4) if (dx, dz) != (0, 0)],
        key=lambda d: -(ring(d[0], X) + abs(d[1])),
    )
    z_offs = sorted(range(1, Z), key=lambda d: -ring(d, Z))
    far_offs = [d for d in z_offs if not (d <= 3 or d >= Z - 4)]
    plane_offs = sorted(
        [(dx, dy) for dx in range(X) for dy in range(Y) if (dx, dy) != (0, 0)],
        key=lambda d: -(ring(d[0], X) + ring(d[1], Y)),
    )

    def at_z(d):
        return place(x, y, (z + d + Z) % Z, c)

    def at_ids(dx, dz):
        return place((x + dx + X) % X, y, (z + dz + Z) % Z, c)

    def at_plane(dx, dy):
        return place((x + dx + X) % X, (y + dy + Y) % Y, z, c)

    q_out = zh * 2 + y // 2
    raw_y = zl // 2
    raw_to = [(q_out + 4 * a) % Z for a in range(4)]
    raw_self = [(raw_y == y) & (raw_to[a] == z) for a in range(4)]
    q_in = z % 4
    raw_from = []
    for h in range(2):
        for m in range(2):
            raw_from.append(((q_in % 2) * 2 + h, (q_in // 2) * ZL + 2 * y + m))
    from_self = [(fy == y) & (fz == z) for fy, fz in raw_from]

    load_grad = pltpu.make_async_copy(grad_ref, grad, load_sem.at[0])
    load_grad.start()
    load = pltpu.make_async_copy(table_ref, table, load_sem.at[1])
    load.start()

    barrier = pltpu.get_barrier_semaphore()
    signal(barrier, twin)
    for d in far_offs:
        signal(barrier, at_z(-d))
    for dx, dz in ids_offs:
        signal(barrier, at_ids(-dx, -dz))
    for dx, dy in plane_offs:
        signal(barrier, at_plane(-dx, -dy))
    for n, (fy, fz) in enumerate(raw_from):
        @pl.when(jnp.logical_not(from_self[n]))
        def _():
            signal(barrier, place(x, fy, fz, c))
    n_self = jnp.where((raw_y == y) & (z % 4 == q_out), 1, 0)

    eye = lax.broadcasted_iota(jnp.int32, (feat, feat), 0) == lax.broadcasted_iota(
        jnp.int32, (feat, feat), 1
    )
    load_grad.wait()
    raw_out[...] = lax.dot_general(
        jnp.where(eye, 1.0, 0.0).astype(BF), grad[...], (((1,), (1,)), ((), ())),
        preferred_element_type=F32,
    ).astype(BF)
    ids_all[dp] = ids_ref[...]
    pl.semaphore_wait(
        barrier, 1 + len(far_offs) + len(ids_offs) + len(plane_offs) + 4 - n_self
    )

    ids_copies = []
    for n, (dx, dz) in enumerate(ids_offs):
        copy = remote(
            ids_ref, ids_all.at[dp], ids_sem.at[0, n], ids_sem.at[1, n], at_ids(dx, dz)
        )
        copy.start()
        ids_copies.append(copy)

    raw_slot = (y % 2) * 2 + zl % 2
    raw_row = pl.multiple_of(((y % 2) * 2 + c) * feat, 16)
    raw_copies = []
    for a in range(4):
        copy = remote(
            raw_out, raw.at[zl % 2, pl.ds(raw_row, feat)],
            raw_sem.at[0, a], raw_sem.at[1, raw_slot],
            place(x, raw_y, raw_to[a], c),
        )
        raw_copies.append(copy)

        @pl.when(jnp.logical_not(raw_self[a]))
        def _(copy=copy):
            copy.start()

        @pl.when(raw_self[a])
        def _():
            raw[zl % 2, pl.ds(raw_row, feat)] = raw_out[...]

    for copy in ids_copies:
        copy.wait_recv()

    for g in range(groups):
        ids_wide[g] = jnp.broadcast_to(ids_all[g], (cap, tok))
    named, local = choose(
        ids_wide[...].reshape(groups * cap, tok), seg * span, span, dp // (groups // PACK), cap
    )
    line = jnp.sum(
        jnp.where(named, (local // PACK + 1).astype(F32), 0.0), axis=1, keepdims=True
    ).astype(jnp.int32) - 1
    hot_ref[...] = jnp.where(
        lax.broadcasted_iota(jnp.int32, (groups * cap, lines), 1) == line, 1.0, 0.0
    ).astype(BF)
    load.wait()

    cuts = [(0, 4), (4, blocks)]
    fwd = []
    for p, (lo, hi) in enumerate(cuts):
        got = jnp.dot(
            hot_ref[...], table[:, lo * LANE:hi * LANE], preferred_element_type=F32
        ).astype(BF)
        for g in range(groups):
            gx, j = g // ZL, g % ZL
            for b in range(lo, hi):
                core = (j - b) % ZL
                rows_out[gx * Y + core // 2, b, core % 2] = got[
                    g * cap:(g + 1) * cap, (b - lo) * LANE:(b - lo + 1) * LANE
                ]
        sent = []
        for n, (dx, dy) in enumerate(plane_offs):
            to = ((x + dx) % X) * Y + (y + dy) % Y
            copy = remote(
                rows_out.at[to, pl.ds(lo, hi - lo)], rows_in.at[mine, pl.ds(lo, hi - lo)],
                fwd_sem.at[0, n, p], fwd_sem.at[1, n, p], at_plane(dx, dy),
            )
            copy.start()
            sent.append(copy)
        fwd.append(sent)
        rows_in[mine, lo:hi] = rows_out[mine, lo:hi]

    slots = X * Y * cap
    bucket = lax.broadcasted_iota(jnp.int32, (slots, tok), 0) // cap
    bucket_first = (zh * ZL + (bucket % Y) * 2 + c) * span
    bucket_slot = (bucket // Y) * 2 + zl // 4
    for m in range(ZL):
        ids = jnp.broadcast_to(ids_all[x * ZL + (2 * y + m) % ZL], (slots, tok))
        hit, _ = choose(ids, bucket_first, span, bucket_slot, cap)
        hit = jnp.where(hit, 1.0, 0.0)
        if m < 2:
            pick[m] = hit.astype(BF)
        scatter[m] = hit.T.astype(BF)

    def merge(p):
        lo, hi = cuts[p]
        for copy in fwd[p]:
            copy.wait_recv()
        for side in range(2):
            for b in range(lo, hi):
                part[side, b] = jnp.dot(
                    scatter[(side + b) % ZL],
                    rows_in[:, b, side].reshape(slots, LANE),
                    preferred_element_type=F32,
                ).astype(BF)
        copy = remote(
            part.at[1 - c, pl.ds(lo, hi - lo)], halves.at[pl.ds(lo, hi - lo)],
            half_sem.at[0, p], half_sem.at[1, p], twin,
        )
        copy.start()
        return copy

    z_copies = []
    my_block = (zl - k + ZL) % ZL
    has_block = my_block < blocks
    for d in z_offs:
        block = (z + d - k + Z) % ZL
        copy = remote(
            sums.at[jnp.minimum(block, blocks - 1)], zin.at[z],
            z_sem.at[0, d], z_sem.at[1, d], at_z(d),
        )
        z_copies.append((block, copy))

    def send_z(p, copy):
        lo, hi = cuts[p]
        copy.wait_recv()
        for b in range(lo, hi):
            sums[b] = part[c, b] + halves[b]
        for block, z_copy in z_copies:
            @pl.when((block >= lo) & (block < hi))
            def _(z_copy=z_copy):
                z_copy.start()

    twin0 = merge(0)

    twin_copies = []
    for n in range(4):
        h, m = n // 2, n % 2
        rows = pl.ds(pl.multiple_of((h * 2 + c) * feat, 16), feat)

        @pl.when(jnp.logical_not(from_self[n]))
        def _(n=n, rows=rows, m=m):
            remote(
                raw_out, raw.at[m, rows], raw_sem.at[0, 0], raw_sem.at[1, n], twin
            ).wait_recv()
        copy = remote(
            raw.at[m, rows], raw.at[m, rows], twin_sem.at[0, n], twin_sem.at[1, n], twin
        )
        copy.start()
        twin_copies.append(copy)

    send_z(0, twin0)
    for copy in twin_copies:
        copy.wait_recv()
    for m in range(2):
        got = lax.dot_general(
            pick[m], raw[m], (((1,), (1,)), ((), ())), preferred_element_type=F32
        ).astype(BF)
        back_out[:, m] = got.reshape(X * Y, cap, width)
    bwd = []
    for n, (dx, dy) in enumerate(plane_offs):
        to = ((x + dx) % X) * Y + (y + dy) % Y
        copy = remote(
            back_out.at[to], back_ref.at[mine], bwd_sem.at[0, n], bwd_sem.at[1, n],
            at_plane(dx, dy),
        )
        copy.start()
        bwd.append(copy)
    back_ref[mine] = back_out[mine]

    twin1 = merge(1)
    send_z(1, twin1)

    def columns(block, q):
        return pl.ds(pl.multiple_of(q * width + block * LANE, LANE), LANE)

    @pl.when(has_block)
    def _():
        zin[z] = sums[my_block]
        for _, copy in z_copies:
            copy.wait_recv()

    ag = []
    for q in range(4):
        cols = columns(jnp.minimum(my_block, blocks - 1), q)
        for dy in range(Y):
            if dy == 0:
                peer, sem = twin, rel_sem
            else:
                peer, sem = at_plane(0, dy), ag_sem
            ag.append(remote(
                emb_ref.at[:, cols], emb_ref.at[:, cols],
                sem.at[0, dy, q], sem.at[1, dy, q], peer,
            ))

    @pl.when(has_block)
    def _():
        for q in range(4):
            cols = columns(my_block, q)
            emb_ref[:, cols] = (zin[q] + zin[q + 4]) + (zin[q + 8] + zin[q + 12])
            for dy in (2, 1, 3, 0):
                ag[q * Y + dy].start()

    relays = []
    for dy in (1, 3, 2):
        from_k = 2 * ((y - dy + Y) % Y) + c
        from_block = (zl - from_k + ZL) % ZL
        for q in range(4):
            cols = columns(jnp.minimum(from_block, blocks - 1), q)
            relay = remote(
                emb_ref.at[:, cols], emb_ref.at[:, cols],
                rel_sem.at[0, dy, q], rel_sem.at[1, dy, q], twin,
            )
            relays.append((from_block, relay))

            @pl.when(from_block < blocks)
            def _(relay=relay, copy=ag[q * Y + dy]):
                copy.wait_recv()
                relay.start()

    for copy in bwd:
        copy.wait_recv()

    for dy in range(Y):
        other_k = 2 * ((y - dy + Y) % Y) + 1 - c
        other_block = (zl - other_k + ZL) % ZL

        @pl.when(other_block < blocks)
        def _(dy=dy):
            for q in range(4):
                remote(
                    emb_ref.at[:, columns(0, q)], emb_ref.at[:, columns(0, q)],
                    rel_sem.at[0, dy, q], rel_sem.at[1, dy, q], twin,
                ).wait_recv()

    for copies in [ids_copies, twin_copies, bwd, [twin0, twin1]] + fwd:
        for copy in copies:
            copy.wait_send()
    for a in range(4):
        @pl.when(jnp.logical_not(raw_self[a]))
        def _(a=a):
            raw_copies[a].wait_send()
    for block, copy in z_copies:
        @pl.when(block < blocks)
        def _(copy=copy):
            copy.wait_send()

    @pl.when(has_block)
    def _():
        for copy in ag:
            copy.wait_send()
    for from_block, relay in relays:
        @pl.when(from_block < blocks)
        def _(relay=relay):
            relay.wait_send()


def body(token_ids, table, out_grad, groups, segs):
    lines, width = table.shape
    tok, piece = out_grad.shape
    depth = segs * piece
    cap = tok // PACK
    blocks = width // LANE
    vmem = pl.BlockSpec(memory_space=pltpu.VMEM)
    hbm = pl.BlockSpec(memory_space=pltpu.HBM)
    dma = pltpu.SemaphoreType.DMA
    emb, back, hot = pl.pallas_call(
        kernel,
        out_shape=(
            jax.ShapeDtypeStruct((tok, depth), BF),
            jax.ShapeDtypeStruct((X * Y, 2, cap, width), BF),
            jax.ShapeDtypeStruct((groups * cap, lines), BF),
        ),
        in_specs=[vmem, hbm, hbm],
        out_specs=(vmem, vmem, vmem),
        scratch_shapes=[
            pltpu.VMEM((groups, 1, tok), jnp.int32),
            pltpu.VMEM((groups, cap, tok), jnp.int32),
            pltpu.VMEM((lines, width), BF),
            pltpu.VMEM((tok, piece), BF),
            pltpu.VMEM((piece, tok), BF),
            pltpu.VMEM((2, width, tok), BF),
            pltpu.VMEM((X * Y, blocks, 2, cap, LANE), BF),
            pltpu.VMEM((X * Y, blocks, 2, cap, LANE), BF),
            pltpu.VMEM((2, X * Y * cap, tok), BF),
            pltpu.VMEM((ZL, tok, X * Y * cap), BF),
            pltpu.VMEM((2, blocks, tok, LANE), BF),
            pltpu.VMEM((blocks, tok, LANE), BF),
            pltpu.VMEM((blocks, tok, LANE), BF),
            pltpu.VMEM((Z, tok, LANE), BF),
            pltpu.VMEM((X * Y, 2, cap, width), BF),
            dma((2,)),
            dma((2, groups)),
            dma((2, 4)),
            dma((2, 4)),
            dma((2, X * Y, 2)),
            dma((2, 2)),
            dma((2, Z)),
            dma((2, X * Y)),
            dma((2, Y, 4)),
            dma((2, Y, 4)),
        ],
        compiler_params=pltpu.CompilerParams(
            collective_id=0, has_side_effects=True, vmem_limit_bytes=48 << 20
        ),
    )(token_ids[None, :], table, out_grad)
    grad = lax.dot_general(
        hot, back.reshape(groups * cap, width), (((0,), (0,)), ((), ())),
        preferred_element_type=F32,
    )
    return emb, grad.astype(BF)


def solution(mesh):
    placed = (P("dp"), P("segment", "dp"), P("dp", "segment"))
    return jax.shard_map(
        functools.partial(body, groups=mesh.shape["dp"], segs=mesh.shape["segment"]),
        mesh=mesh,
        in_specs=placed,
        out_specs=(P("dp", None), P("segment", "dp")),
        check_vma=False,
    )
```

time: 217 us -> 84.7 us (0.39)
  the two profiles are of different devices: /device:TPU:131 before, /device:TPU:1 now
where the time goes in v1:
time: 84.7 us; the launch traced here: 84.5 us
  Pallas kernels  77 us (91%)
  local copies, waits for them, and re-layouts  4.09 us (5%)
  matrix products  2.8 us (3%)
    pallas_call x1, Pallas kernels, body(): pl.pallas_call(kernel, out_shape=(jax.ShapeDtypeStruct((tok, depth), BF),...  77 us
    unnamed x6, local copies, waits for them, and re-layouts  4.09 us
    dot_general x1, matrix products, body(): lax.dot_general(hot, back.reshape(groups * cap, width), (((0,), (0,)), ((...  2.8 us

profile of v1, /device:TPU:1, one launch (start us, length us, event | category | flops | bytes accessed | tf_op | source)
XLA Modules:
  0.0 84.5 jit_solution(15890872774395899419)
XLA Ops:
  0.6 0.9 %copy.5.grad_ref = bf16[128,224]{1,0:T(8,128)(2,1)S(1)} copy(bf16[128,224]{0,1:T(8,128)(2,1)} %param.5) | data formatting | bytes 114688 | tf_op args[2]
  1.6 0.0 copy-start
  1.6 1.6 %copy-done = bf16[1188,896]{1,0:T(8,128)(2,1)S(1)} copy-done((bf16[1188,896]{1,0:T(8,128)(2,1)S(1)}, bf16[1188,896]{1,0:T(8,128)(2,1)}, u32[]{:S(2)}) %copy-start) | copy-done | bytes 2128920
  3.2 0.0 copy-start.1
  3.2 0.7 copy-done.1
  3.8 77.0 %shard_map.50 = (bf16[128,3584]{1,0:T(8,128)(2,1)S(1)}, bf16[16,2,16,896]{3,2,1,0:T(8,128)(2,1)S(1)}, bf16[512,1188]{1,0:T(8,128)(2,1)S(1)}) custom-call(s32[1,128]{1,0:T(1,128)S(1)} %bitcast.4, bf16[1188,896]{1,0:T(8,128)(2,1)S(1)} %copy-done, bf16[128,224]{1,0:T(8,128)(2,1)S(1)} %copy.5.grad_ref), custom_call_target="tpu_custom_call" | custom-call | tf_op jit(solution)/shard_map/pallas_call | solution.py:395
  80.8 2.8 %convolution_convert_fusion = bf16[1188,896]{1,0:T(8,128)(2,1)} fusion(bf16[512,1188]{1,0:T(8,128)(2,1)S(1)} %get-tuple-element.6, bf16[512,896]{1,0:T(8,128)(2,1)S(1)} %bitcast.5), kind=kOutput, calls=%fused_computation | convolution fusion | flops 1091059200 | bytes 4262912 | tf_op jit(solution)/shard_map/dot_general | solution.py:435
  83.6 0.9 %copy.7 = bf16[128,3584]{1,0:T(8,128)(2,1)} copy(bf16[128,3584]{1,0:T(8,128)(2,1)S(1)} %get-tuple-element.10) | data formatting | bytes 1835008
Async XLA Ops:
  1.6 1.6 %copy-start = (bf16[1188,896]{1,0:T(8,128)(2,1)S(1)}, bf16[1188,896]{1,0:T(8,128)(2,1)}, u32[]{:S(2)}) copy-start(bf16[1188,896]{1,0:T(8,128)(2,1)} %table_ref.1) | copy-start | bytes 6386692
  3.2 0.7 copy-start.1

commit v2 on v1

v2 whole, which is shorter than its diff:
```python
import functools

import jax
import jax.numpy as jnp
from jax import lax
from jax.experimental import pallas as pl
from jax.experimental.pallas import tpu as pltpu
from jax.sharding import PartitionSpec as P

PACK = 8
BF = jnp.bfloat16
F32 = jnp.float32
MESH = pl.DeviceIdType.MESH

X, Y, Z, ZL = 4, 4, 16, 8
LANE = 128


def place(x, y, z, c):
    return {"segment": (z // ZL) * ZL + y * 2 + c, "dp": x * ZL + z % ZL}


def remote(src, dst, send, recv, peer):
    return pltpu.make_async_remote_copy(
        src_ref=src, dst_ref=dst, send_sem=send, recv_sem=recv,
        device_id=peer, device_id_type=MESH,
    )


def signal(sem, peer):
    pl.semaphore_signal(sem, inc=1, device_id=peer, device_id_type=MESH)


def ring(d, n):
    return min(d % n, n - d % n)


def choose(ids, first, span, slot, cap):
    rows, tok = ids.shape
    local = ids - first
    owned = (local >= 0) & (local < span) & ((ids & (PACK - 1)) == slot)
    before = lax.broadcasted_iota(jnp.int32, (tok, tok), 0) < lax.broadcasted_iota(
        jnp.int32, (tok, tok), 1
    )
    rank = jnp.dot(
        jnp.where(owned, 1.0, 0.0).astype(BF),
        jnp.where(before, 1.0, 0.0).astype(BF),
        preferred_element_type=F32,
    )
    want = lax.broadcasted_iota(jnp.int32, (rows, tok), 0) % cap
    return owned & (rank.astype(jnp.int32) == want), local


def kernel(
    ids_ref, table_ref, grad_ref,
    emb_ref, out_ref,
    ids_all, ids_wide, table, raw_out, raw_row, raw, rows_out, rows_in, pick, scatter,
    part, halves, sums, inbox, outbox, zin, back_out, back, hot,
    load_sem, ids_sem, row_sem, raw_sem, twin_sem, fwd_sem, half_sem, near_sem, z_sem, bwd_sem,
    ag_sem, rel_sem,
):
    seg = lax.axis_index("segment")
    dp = lax.axis_index("dp")
    c = seg % 2
    y = (seg // 2) % Y
    zh = seg // ZL
    zl = dp % ZL
    z = zh * ZL + zl
    x = dp // ZL
    mine = x * Y + y
    k = 2 * y + c
    lines, width = table.shape
    tok = ids_ref.shape[1]
    feat = raw_out.shape[0]
    groups = X * ZL
    cap = rows_in.shape[3]
    blocks = width // LANE
    span = lines * PACK
    twin = place(x, y, z, 1 - c)

    ids_offs = sorted(
        [(dx, dz) for dx in range(X) for dz in range(-4, 4) if (dx, dz) != (0, 0)],
        key=lambda d: -(ring(d[0], X) + abs(d[1])),
    )
    plane_offs = sorted(
        [(dx, dy) for dx in range(X) for dy in range(Y) if (dx, dy) != (0, 0)],
        key=lambda d: -(ring(d[0], X) + ring(d[1], Y)),
    )

    turn = 1 - 2 * c

    def along(d):
        return (z + turn * d + 2 * Z) % Z

    def at_z(d):
        return place(x, y, along(d), c)

    def at_ids(dx, dz):
        return place((x + dx + X) % X, y, (z + dz + Z) % Z, c)

    def at_plane(dx, dy):
        return place((x + dx + X) % X, (y + dy + Y) % Y, z, c)

    raw_to = [4 * ((y - zl // 2 - 2 * u + 8) % 4) + 2 * zh + u for u in range(2)]
    pair = (y - z // 4 - 2 * (z % 2) + 8) % 4
    raw_from = [(z % 4) // 2 * ZL + 2 * pair + m for m in range(2)]

    load_grad = pltpu.make_async_copy(grad_ref, raw_out, load_sem.at[0])
    load_grad.start()
    load = pltpu.make_async_copy(table_ref, table, load_sem.at[1])
    load.start()

    barrier = pltpu.get_barrier_semaphore()
    signal(barrier, twin)
    signal(barrier, at_ids(0, -4))
    for dx, dz in ids_offs:
        signal(barrier, at_ids(-dx, -dz))
    for dx, dy in plane_offs:
        signal(barrier, at_plane(-dx, -dy))
    for m in range(2):
        @pl.when(raw_from[m] != z)
        def _(m=m):
            signal(barrier, place(x, y, raw_from[m], c))
    n_raw = sum(jnp.where(raw_to[u] != z, 1, 0) for u in range(2))

    ids_all[dp] = ids_ref[...]
    pl.semaphore_wait(
        barrier, 2 + len(ids_offs) + len(plane_offs) + n_raw
    )

    ids_copies = []
    for n, (dx, dz) in enumerate(ids_offs):
        copy = remote(
            ids_ref, ids_all.at[dp], ids_sem.at[0, n], ids_sem.at[1, n], at_ids(dx, dz)
        )
        copy.start()
        ids_copies.append(copy)

    load_grad.wait()
    rows_sent = []
    for dy in (2, 1, 3):
        copy = remote(
            raw_out, raw_row.at[y], row_sem.at[0, dy], row_sem.at[1, dy], at_plane(0, dy)
        )
        copy.start()
        rows_sent.append(copy)
    raw_row[y] = raw_out[...]

    for copy in ids_copies:
        copy.wait_recv()

    for copy in rows_sent:
        copy.wait_recv()
    raw_copies = []
    for u in range(2):
        for v in range(2):
            rows = pl.ds(pl.multiple_of((v * 2 + c) * feat, 16), feat)
            copy = remote(
                raw_row.at[2 * u + v], raw.at[zl % 2, rows],
                raw_sem.at[0, 2 * u + v], raw_sem.at[1, v * 2 + zl % 2],
                place(x, y, raw_to[u], c),
            )
            raw_copies.append((u, copy))

            @pl.when(raw_to[u] != z)
            def _(copy=copy):
                copy.start()

            @pl.when(raw_to[u] == z)
            def _(u=u, v=v, rows=rows):
                raw[zl % 2, rows] = raw_row[2 * u + v]

    for g in range(groups):
        ids_wide[g] = jnp.broadcast_to(ids_all[g], (cap, tok))
    named, local = choose(
        ids_wide[...].reshape(groups * cap, tok), seg * span, span, dp // (groups // PACK), cap
    )
    line = jnp.sum(
        jnp.where(named, (local // PACK + 1).astype(F32), 0.0), axis=1, keepdims=True
    ).astype(jnp.int32) - 1
    hot[...] = jnp.where(
        lax.broadcasted_iota(jnp.int32, (groups * cap, lines), 1) == line, 1.0, 0.0
    ).astype(BF)
    load.wait()

    cuts = [(0, 4), (4, blocks)]
    fwd = []
    for p, (lo, hi) in enumerate(cuts):
        got = jnp.dot(
            hot[...], table[:, lo * LANE:hi * LANE], preferred_element_type=F32
        ).astype(BF)
        for g in range(groups):
            gx, j = g // ZL, g % ZL
            for b in range(lo, hi):
                core = (j - b) % ZL
                rows_out[gx * Y + core // 2, b, core % 2] = got[
                    g * cap:(g + 1) * cap, (b - lo) * LANE:(b - lo + 1) * LANE
                ]
        sent = []
        for n, (dx, dy) in enumerate(plane_offs):
            to = ((x + dx) % X) * Y + (y + dy) % Y
            copy = remote(
                rows_out.at[to, pl.ds(lo, hi - lo)], rows_in.at[mine, pl.ds(lo, hi - lo)],
                fwd_sem.at[0, n, p], fwd_sem.at[1, n, p], at_plane(dx, dy),
            )
            copy.start()
            sent.append(copy)
        fwd.append(sent)
        rows_in[mine, lo:hi] = rows_out[mine, lo:hi]

    slots = X * Y * cap
    bucket = lax.broadcasted_iota(jnp.int32, (slots, tok), 0) // cap
    bucket_first = (zh * ZL + (bucket % Y) * 2 + c) * span
    bucket_slot = (bucket // Y) * 2 + zl // 4
    for m in range(ZL):
        ids = jnp.broadcast_to(ids_all[x * ZL + m], (slots, tok))
        hit, _ = choose(ids, bucket_first, span, bucket_slot, cap)
        hit = jnp.where(hit, 1.0, 0.0)
        pick[m] = hit.astype(BF)
        scatter[m] = hit.T.astype(BF)

    def merge(p):
        lo, hi = cuts[p]
        for copy in fwd[p]:
            copy.wait_recv()
        for side in range(2):
            for b in range(lo, hi):
                part[side, b] = jnp.dot(
                    scatter[(2 * y + side + b) % ZL],
                    rows_in[:, b, side].reshape(slots, LANE),
                    preferred_element_type=F32,
                ).astype(BF)
        copy = remote(
            part.at[1 - c, pl.ds(lo, hi - lo)], halves.at[pl.ds(lo, hi - lo)],
            half_sem.at[0, p], half_sem.at[1, p], twin,
        )
        copy.start()
        return copy

    def block_of(d):
        return (along(d) - k + Z) % ZL

    def within(block, p):
        return (block >= cuts[p][0]) & (block < cuts[p][1])

    my_block = block_of(0)
    has_block = my_block < blocks
    steps = [(0, d) for d in range(4)] + [(1, -d) for d in range(1, 5)]
    near = []
    for n, (way, d) in enumerate(steps):
        block = block_of(d + (-4 if way else 4))
        near.append((block, remote(
            sums.at[jnp.minimum(block, blocks - 1)], inbox.at[n],
            near_sem.at[0, n], near_sem.at[1, n], at_z(-4 if way else 4),
        )))
    z_copies = []
    for n, (way, d) in enumerate(steps):
        z_copies.append((block_of(d), None if d == 0 else remote(
            outbox.at[n], zin.at[way, z % 4], z_sem.at[0, n], z_sem.at[1, n], at_z(d),
        )))
    order = sorted(range(8), key=lambda n: -abs(steps[n][1]))

    def send_z(p, copy):
        lo, hi = cuts[p]
        copy.wait_recv()
        for b in range(lo, hi):
            sums[b] = part[c, b] + halves[b]
        for n in order:
            block, near_copy = near[n]

            @pl.when(within(block, p))
            def _(near_copy=near_copy):
                near_copy.start()

    def pass_z(p):
        for n in order:
            block, z_copy = z_copies[n]

            @pl.when(within(block, p))
            def _(n=n, block=block, z_copy=z_copy):
                near[n][1].wait_recv()
                both = sums[block] + inbox[n]
                if steps[n][1] == 0:
                    zin[0, z % 4] = both
                else:
                    outbox[n] = both
                    z_copy.start()

    twin0 = merge(0)

    send_z(0, twin0)
    twin1 = merge(1)
    send_z(1, twin1)

    twin_copies = []
    for n in range(4):
        v, m = n // 2, n % 2
        rows = pl.ds(pl.multiple_of((v * 2 + c) * feat, 16), feat)
        copy = remote(
            raw.at[m, rows], raw.at[m, rows], twin_sem.at[0, n], twin_sem.at[1, n], twin
        )

        @pl.when(raw_from[m] != z)
        def _(n=n, m=m, rows=rows):
            remote(
                raw_out, raw.at[m, rows], raw_sem.at[0, 0], raw_sem.at[1, n], twin
            ).wait_recv()
        copy.start()
        twin_copies.append(copy)

    for copy in twin_copies:
        copy.wait_recv()
    for m in range(2):
        got = lax.dot_general(
            pick[2 * pair + m], raw[m], (((1,), (1,)), ((), ())), preferred_element_type=F32
        ).astype(BF)
        back_out[:, m] = got.reshape(X * Y, cap, width)
    bwd = []
    for n, (dx, dy) in enumerate(plane_offs):
        to = ((x + dx) % X) * Y + (y + dy) % Y
        copy = remote(
            back_out.at[to], back.at[x * Y + pair], bwd_sem.at[0, n], bwd_sem.at[1, n],
            at_plane(dx, dy),
        )
        copy.start()
        bwd.append(copy)
    back[x * Y + pair] = back_out[mine]

    pass_z(0)
    pass_z(1)

    def columns(block, q):
        return pl.ds(pl.multiple_of(q * width + block * LANE, LANE), LANE)

    def quarter(d):
        return (along(-d)) % 4

    ag = []
    for d in range(4):
        cols = columns(jnp.minimum(my_block, blocks - 1), quarter(d))
        for dy in range(Y):
            if dy == 0:
                peer, sem = twin, rel_sem
            else:
                peer, sem = at_plane(0, dy), ag_sem
            ag.append(remote(
                emb_ref.at[:, cols], emb_ref.at[:, cols],
                sem.at[0, dy, d], sem.at[1, dy, d], peer,
            ))

    @pl.when(has_block)
    def _():
        for d in range(4):
            if d > 0:
                z_copies[d][1].wait_recv()
            z_copies[3 + 4 - d][1].wait_recv()
            cols = columns(my_block, quarter(d))
            emb_ref[:, cols] = zin[0, quarter(d)] + zin[1, quarter(d)]
            for dy in (2, 1, 3, 0):
                ag[d * Y + dy].start()

    for copy in bwd:
        copy.wait_recv()
    out_ref[...] = lax.dot_general(
        hot[...], back[...].reshape(groups * cap, width), (((0,), (0,)), ((), ())),
        preferred_element_type=F32,
    ).astype(BF)

    relays = []
    for dy in (1, 3, 2):
        from_k = 2 * ((y - dy + Y) % Y) + c
        from_block = (zl - from_k + ZL) % ZL
        for q in range(4):
            cols = columns(jnp.minimum(from_block, blocks - 1), quarter(q))
            relay = remote(
                emb_ref.at[:, cols], emb_ref.at[:, cols],
                rel_sem.at[0, dy, q], rel_sem.at[1, dy, q], twin,
            )
            relays.append((from_block, relay))

            @pl.when(from_block < blocks)
            def _(relay=relay, copy=ag[q * Y + dy]):
                copy.wait_recv()
                relay.start()

    for dy in range(Y):
        other_k = 2 * ((y - dy + Y) % Y) + 1 - c
        other_block = (zl - other_k + ZL) % ZL

        @pl.when(other_block < blocks)
        def _(dy=dy):
            for q in range(4):
                remote(
                    emb_ref.at[:, columns(0, q)], emb_ref.at[:, columns(0, q)],
                    rel_sem.at[0, dy, q], rel_sem.at[1, dy, q], twin,
                ).wait_recv()

    for copies in [ids_copies, rows_sent, twin_copies, bwd, [twin0, twin1]] + fwd:
        for copy in copies:
            copy.wait_send()
    for u, copy in raw_copies:
        @pl.when(raw_to[u] != z)
        def _(copy=copy):
            copy.wait_send()
    for block, copy in near:
        @pl.when(block < blocks)
        def _(copy=copy):
            copy.wait_send()
    for block, copy in z_copies[1:]:
        @pl.when(block < blocks)
        def _(copy=copy):
            copy.wait_send()

    @pl.when(has_block)
    def _():
        for copy in ag:
            copy.wait_send()
    for from_block, relay in relays:
        @pl.when(from_block < blocks)
        def _(relay=relay):
            relay.wait_send()


def body(token_ids, table, out_grad, groups, segs):
    lines, width = table.shape
    tok, piece = out_grad.shape
    depth = segs * piece
    cap = tok // PACK
    blocks = width // LANE
    vmem = pl.BlockSpec(memory_space=pltpu.VMEM)
    hbm = pl.BlockSpec(memory_space=pltpu.HBM)
    dma = pltpu.SemaphoreType.DMA
    return pl.pallas_call(
        kernel,
        out_shape=(
            jax.ShapeDtypeStruct((tok, depth), BF),
            jax.ShapeDtypeStruct((lines, width), BF),
        ),
        in_specs=[vmem, hbm, hbm],
        out_specs=(vmem, vmem),
        scratch_shapes=[
            pltpu.VMEM((groups, 1, tok), jnp.int32),
            pltpu.VMEM((groups, cap, tok), jnp.int32),
            pltpu.VMEM((lines, width), BF),
            pltpu.VMEM((piece, tok), BF),
            pltpu.VMEM((Y, piece, tok), BF),
            pltpu.VMEM((2, width, tok), BF),
            pltpu.VMEM((X * Y, blocks, 2, cap, LANE), BF),
            pltpu.VMEM((X * Y, blocks, 2, cap, LANE), BF),
            pltpu.VMEM((ZL, X * Y * cap, tok), BF),
            pltpu.VMEM((ZL, tok, X * Y * cap), BF),
            pltpu.VMEM((2, blocks, tok, LANE), BF),
            pltpu.VMEM((blocks, tok, LANE), BF),
            pltpu.VMEM((blocks, tok, LANE), BF),
            pltpu.VMEM((8, tok, LANE), BF),
            pltpu.VMEM((8, tok, LANE), BF),
            pltpu.VMEM((2, 4, tok, LANE), BF),
            pltpu.VMEM((X * Y, 2, cap, width), BF),
            pltpu.VMEM((X * Y, 2, cap, width), BF),
            pltpu.VMEM((groups * cap, lines), BF),
            dma((2,)),
            dma((2, groups)),
            dma((2, Y)),
            dma((2, 4)),
            dma((2, 4)),
            dma((2, X * Y, 2)),
            dma((2, 2)),
            dma((2, 8)),
            dma((2, 8)),
            dma((2, X * Y)),
            dma((2, Y, 4)),
            dma((2, Y, 4)),
        ],
        compiler_params=pltpu.CompilerParams(
            collective_id=0, has_side_effects=True, vmem_limit_bytes=50 << 20
        ),
    )(token_ids[None, :], table, out_grad.T)


def solution(mesh):
    placed = (P("dp"), P("segment", "dp"), P("dp", "segment"))
    return jax.shard_map(
        functools.partial(body, groups=mesh.shape["dp"], segs=mesh.shape["segment"]),
        mesh=mesh,
        in_specs=placed,
        out_specs=(P("dp", None), P("segment", "dp")),
        check_vma=False,
    )
```

time: 84.7 us -> 70.7 us (0.83)
  Pallas kernels: 77 us -> 66.2 us
  matrix products: 2.8 us -> 0 us
    pallas_call x1, Pallas kernels: 77 us -> 66.2 us  [body(): pl.pallas_call(kernel, out_shape=(jax.ShapeDtypeStruct((tok, depth), BF),...]
    dot_general x1 -> x0, matrix products: 2.8 us -> none  [body(): lax.dot_general(hot, back.reshape(groups * cap, width), (((0,), (0,)), ((...]
where the time goes in v2:
time: 70.7 us; the launch traced here: 70.6 us
  Pallas kernels  66.2 us (94%)
  local copies, waits for them, and re-layouts  3.72 us (5%)
    pallas_call x1, Pallas kernels, body(): pl.pallas_call(kernel, out_shape=(jax.ShapeDtypeStruct((tok, depth), BF),...  66.2 us
    unnamed x6, local copies, waits for them, and re-layouts  3.72 us

profile of v2, /device:TPU:1, one launch (start us, length us, event | category | flops | bytes accessed | tf_op | source)
XLA Modules:
  0.0 70.6 jit_solution(1643113662826293227)
XLA Ops:
  0.6 0.0 copy-start
  0.6 0.8 %copy-done = bf16[128,224]{0,1:T(8,128)(2,1)S(1)} copy-done((bf16[128,224]{0,1:T(8,128)(2,1)S(1)}, bf16[128,224]{0,1:T(8,128)(2,1)}, u32[]{:S(2)}) %copy-start) | copy-done | bytes 57368
  1.4 0.0 copy-start.1
  1.5 0.7 copy-done.1
  2.1 66.2 %shard_map.50 = (bf16[128,3584]{1,0:T(8,128)(2,1)S(1)}, bf16[1188,896]{1,0:T(8,128)(2,1)S(1)}) custom-call(s32[1,128]{1,0:T(1,128)S(1)} %bitcast.3, bf16[1188,896]{1,0:T(8,128)(2,1)} %table_ref.1, bf16[224,128]{1,0:T(8,128)(2,1)S(1)} %bitcast.2), custom_call_target="tpu_custom_call" | custom-call | tf_op jit(solution)/shard_map/pallas_call | solution.py:433
  68.3 0.9 %copy.7 = bf16[128,3584]{1,0:T(8,128)(2,1)} copy(bf16[128,3584]{1,0:T(8,128)(2,1)S(1)} %get-tuple-element.4) | data formatting | bytes 1835008
  69.2 1.3 %copy.8 = bf16[1188,896]{1,0:T(8,128)(2,1)} copy(bf16[1188,896]{1,0:T(8,128)(2,1)S(1)} %get-tuple-element.5) | data formatting | bytes 4257792
Async XLA Ops:
  0.6 0.8 %copy-start = (bf16[128,224]{0,1:T(8,128)(2,1)S(1)}, bf16[128,224]{0,1:T(8,128)(2,1)}, u32[]{:S(2)}) copy-start(bf16[128,224]{0,1:T(8,128)(2,1)} %param.5) | copy-start | bytes 172036
  1.4 0.7 copy-start.1

commit v3 on v2

--- a/solution.py
+++ b/solution.py
@@ -27,6 +27,14 @@
     )
 
 
+def arrived(ref, sem, peer):
+    remote(ref, ref, sem, sem, peer).wait_recv()
+
+
+def left(ref, sem, peer):
+    remote(ref, ref, sem, sem, peer).wait_send()
+
+
 def signal(sem, peer):
     pl.semaphore_signal(sem, inc=1, device_id=peer, device_id_type=MESH)
 
@@ -52,9 +60,9 @@
 
 
 def kernel(
-    ids_ref, table_ref, grad_ref,
+    ids_hbm, table_ref, grad_ref,
     emb_ref, out_ref,
-    ids_all, ids_wide, table, raw_out, raw_row, raw, rows_out, rows_in, pick, scatter,
+    ids_ref, ids_all, ids_wide, table, raw_out, raw_row, raw, rows_out, rows_in, pick, scatter,
     part, halves, sums, inbox, outbox, zin, back_out, back, hot,
     load_sem, ids_sem, row_sem, raw_sem, twin_sem, fwd_sem, half_sem, near_sem, z_sem, bwd_sem,
     ag_sem, rel_sem,
@@ -105,6 +113,8 @@
     pair = (y - z // 4 - 2 * (z % 2) + 8) % 4
     raw_from = [(z % 4) // 2 * ZL + 2 * pair + m for m in range(2)]
 
+    load_ids = pltpu.make_async_copy(ids_hbm, ids_ref, load_sem.at[2])
+    load_ids.start()
     load_grad = pltpu.make_async_copy(grad_ref, raw_out, load_sem.at[0])
     load_grad.start()
     load = pltpu.make_async_copy(table_ref, table, load_sem.at[1])
@@ -123,44 +133,33 @@
             signal(barrier, place(x, y, raw_from[m], c))
     n_raw = sum(jnp.where(raw_to[u] != z, 1, 0) for u in range(2))
 
+    load_ids.wait()
     ids_all[dp] = ids_ref[...]
     pl.semaphore_wait(
         barrier, 2 + len(ids_offs) + len(plane_offs) + n_raw
     )
 
-    ids_copies = []
-    for n, (dx, dz) in enumerate(ids_offs):
-        copy = remote(
-            ids_ref, ids_all.at[dp], ids_sem.at[0, n], ids_sem.at[1, n], at_ids(dx, dz)
-        )
-        copy.start()
-        ids_copies.append(copy)
+    for dx, dz in ids_offs:
+        remote(
+            ids_ref, ids_all.at[dp], ids_sem.at[0], ids_sem.at[1], at_ids(dx, dz)
+        ).start()
 
     load_grad.wait()
-    rows_sent = []
     for dy in (2, 1, 3):
-        copy = remote(
-            raw_out, raw_row.at[y], row_sem.at[0, dy], row_sem.at[1, dy], at_plane(0, dy)
-        )
-        copy.start()
-        rows_sent.append(copy)
+        remote(
+            raw_out, raw_row.at[y], row_sem.at[0], row_sem.at[1], at_plane(0, dy)
+        ).start()
     raw_row[y] = raw_out[...]
 
-    for copy in ids_copies:
-        copy.wait_recv()
-
-    for copy in rows_sent:
-        copy.wait_recv()
-    raw_copies = []
+    arrived(raw_row.at[pl.ds(0, Y - 1)], row_sem.at[1], twin)
     for u in range(2):
         for v in range(2):
             rows = pl.ds(pl.multiple_of((v * 2 + c) * feat, 16), feat)
             copy = remote(
                 raw_row.at[2 * u + v], raw.at[zl % 2, rows],
-                raw_sem.at[0, 2 * u + v], raw_sem.at[1, v * 2 + zl % 2],
+                raw_sem.at[0, u], raw_sem.at[1, zl % 2],
                 place(x, y, raw_to[u], c),
             )
-            raw_copies.append((u, copy))
 
             @pl.when(raw_to[u] != z)
             def _(copy=copy):
@@ -169,6 +168,8 @@
             @pl.when(raw_to[u] == z)
             def _(u=u, v=v, rows=rows):
                 raw[zl % 2, rows] = raw_row[2 * u + v]
+
+    arrived(ids_all.at[pl.ds(0, groups - 1)], ids_sem.at[1], twin)
 
     for g in range(groups):
         ids_wide[g] = jnp.broadcast_to(ids_all[g], (cap, tok))
@@ -184,7 +185,6 @@
     load.wait()
 
     cuts = [(0, 4), (4, blocks)]
-    fwd = []
     for p, (lo, hi) in enumerate(cuts):
         got = jnp.dot(
             hot[...], table[:, lo * LANE:hi * LANE], preferred_element_type=F32
@@ -196,16 +196,12 @@
                 rows_out[gx * Y + core // 2, b, core % 2] = got[
                     g * cap:(g + 1) * cap, (b - lo) * LANE:(b - lo + 1) * LANE
                 ]
-        sent = []
-        for n, (dx, dy) in enumerate(plane_offs):
+        for dx, dy in plane_offs:
             to = ((x + dx) % X) * Y + (y + dy) % Y
-            copy = remote(
+            remote(
                 rows_out.at[to, pl.ds(lo, hi - lo)], rows_in.at[mine, pl.ds(lo, hi - lo)],
-                fwd_sem.at[0, n, p], fwd_sem.at[1, n, p], at_plane(dx, dy),
-            )
-            copy.start()
-            sent.append(copy)
-        fwd.append(sent)
+                fwd_sem.at[0, p], fwd_sem.at[1, p], at_plane(dx, dy),
+            ).start()
         rows_in[mine, lo:hi] = rows_out[mine, lo:hi]
 
     slots = X * Y * cap
@@ -221,8 +217,7 @@
 
     def merge(p):
         lo, hi = cuts[p]
-        for copy in fwd[p]:
-            copy.wait_recv()
+        arrived(rows_in.at[pl.ds(0, X * Y - 1), pl.ds(lo, hi - lo)], fwd_sem.at[1, p], twin)
         for side in range(2):
             for b in range(lo, hi):
                 part[side, b] = jnp.dot(
@@ -251,12 +246,12 @@
         block = block_of(d + (-4 if way else 4))
         near.append((block, remote(
             sums.at[jnp.minimum(block, blocks - 1)], inbox.at[n],
-            near_sem.at[0, n], near_sem.at[1, n], at_z(-4 if way else 4),
+            near_sem.at[8], near_sem.at[n], at_z(-4 if way else 4),
         )))
     z_copies = []
     for n, (way, d) in enumerate(steps):
         z_copies.append((block_of(d), None if d == 0 else remote(
-            outbox.at[n], zin.at[way, z % 4], z_sem.at[0, n], z_sem.at[1, n], at_z(d),
+            outbox.at[n], zin.at[way, z % 4], z_sem.at[4], z_sem.at[d % 4], at_z(d),
         )))
     order = sorted(range(8), key=lambda n: -abs(steps[n][1]))
 
@@ -292,38 +287,28 @@
     twin1 = merge(1)
     send_z(1, twin1)
 
-    twin_copies = []
-    for n in range(4):
-        v, m = n // 2, n % 2
-        rows = pl.ds(pl.multiple_of((v * 2 + c) * feat, 16), feat)
-        copy = remote(
-            raw.at[m, rows], raw.at[m, rows], twin_sem.at[0, n], twin_sem.at[1, n], twin
-        )
-
+    for m in range(2):
         @pl.when(raw_from[m] != z)
-        def _(n=n, m=m, rows=rows):
+        def _(m=m):
+            arrived(raw_row.at[pl.ds(0, 2)], raw_sem.at[1, m], twin)
+        for v in range(2):
+            rows = pl.ds(pl.multiple_of((v * 2 + c) * feat, 16), feat)
             remote(
-                raw_out, raw.at[m, rows], raw_sem.at[0, 0], raw_sem.at[1, n], twin
-            ).wait_recv()
-        copy.start()
-        twin_copies.append(copy)
-
-    for copy in twin_copies:
-        copy.wait_recv()
+                raw.at[m, rows], raw.at[m, rows], twin_sem.at[0], twin_sem.at[1], twin
+            ).start()
+
+    arrived(raw_row, twin_sem.at[1], twin)
     for m in range(2):
         got = lax.dot_general(
             pick[2 * pair + m], raw[m], (((1,), (1,)), ((), ())), preferred_element_type=F32
         ).astype(BF)
         back_out[:, m] = got.reshape(X * Y, cap, width)
-    bwd = []
-    for n, (dx, dy) in enumerate(plane_offs):
+    for dx, dy in plane_offs:
         to = ((x + dx) % X) * Y + (y + dy) % Y
-        copy = remote(
-            back_out.at[to], back.at[x * Y + pair], bwd_sem.at[0, n], bwd_sem.at[1, n],
+        remote(
+            back_out.at[to], back.at[x * Y + pair], bwd_sem.at[0], bwd_sem.at[1],
             at_plane(dx, dy),
-        )
-        copy.start()
-        bwd.append(copy)
+        ).start()
     back[x * Y + pair] = back_out[mine]
 
     pass_z(0)
@@ -340,48 +325,42 @@
         cols = columns(jnp.minimum(my_block, blocks - 1), quarter(d))
         for dy in range(Y):
             if dy == 0:
-                peer, sem = twin, rel_sem
+                peer, out, sem = twin, rel_sem.at[4], rel_sem
             else:
-                peer, sem = at_plane(0, dy), ag_sem
+                peer, out, sem = at_plane(0, dy), ag_sem.at[0], ag_sem
             ag.append(remote(
                 emb_ref.at[:, cols], emb_ref.at[:, cols],
-                sem.at[0, dy, d], sem.at[1, dy, d], peer,
+                out, sem.at[dy], peer,
             ))
 
     @pl.when(has_block)
     def _():
         for d in range(4):
-            if d > 0:
-                z_copies[d][1].wait_recv()
-            z_copies[3 + 4 - d][1].wait_recv()
+            arrived(outbox.at[pl.ds(0, 2 if d else 1)], z_sem.at[d], twin)
             cols = columns(my_block, quarter(d))
             emb_ref[:, cols] = zin[0, quarter(d)] + zin[1, quarter(d)]
             for dy in (2, 1, 3, 0):
                 ag[d * Y + dy].start()
 
-    for copy in bwd:
-        copy.wait_recv()
+    arrived(back.at[pl.ds(0, X * Y - 1)], bwd_sem.at[1], twin)
     out_ref[...] = lax.dot_general(
         hot[...], back[...].reshape(groups * cap, width), (((0,), (0,)), ((), ())),
         preferred_element_type=F32,
     ).astype(BF)
 
-    relays = []
+    four = emb_ref.at[:, pl.ds(0, 4 * LANE)]
     for dy in (1, 3, 2):
         from_k = 2 * ((y - dy + Y) % Y) + c
         from_block = (zl - from_k + ZL) % ZL
-        for q in range(4):
-            cols = columns(jnp.minimum(from_block, blocks - 1), quarter(q))
-            relay = remote(
-                emb_ref.at[:, cols], emb_ref.at[:, cols],
-                rel_sem.at[0, dy, q], rel_sem.at[1, dy, q], twin,
-            )
-            relays.append((from_block, relay))
-
-            @pl.when(from_block < blocks)
-            def _(relay=relay, copy=ag[q * Y + dy]):
-                copy.wait_recv()
-                relay.start()
+
+        @pl.when(from_block < blocks)
+        def _(dy=dy, from_block=from_block):
+            arrived(four, ag_sem.at[dy], twin)
+            for q in range(4):
+                cols = columns(from_block, q)
+                remote(
+                    emb_ref.at[:, cols], emb_ref.at[:, cols], rel_sem.at[4], rel_sem.at[dy], twin
+                ).start()
 
     for dy in range(Y):
         other_k = 2 * ((y - dy + Y) % Y) + 1 - c
@@ -389,36 +368,51 @@
 
         @pl.when(other_block < blocks)
         def _(dy=dy):
-            for q in range(4):
-                remote(
-                    emb_ref.at[:, columns(0, q)], emb_ref.at[:, columns(0, q)],
-                    rel_sem.at[0, dy, q], rel_sem.at[1, dy, q], twin,
-                ).wait_recv()
-
-    for copies in [ids_copies, rows_sent, twin_copies, bwd, [twin0, twin1]] + fwd:
-        for copy in copies:
-            copy.wait_send()
-    for u, copy in raw_copies:
+            arrived(four, rel_sem.at[dy], twin)
+
+    left(ids_all.at[pl.ds(0, groups - 1)], ids_sem.at[0], twin)
+    left(raw_row.at[pl.ds(0, Y - 1)], row_sem.at[0], twin)
+    for u in range(2):
         @pl.when(raw_to[u] != z)
-        def _(copy=copy):
-            copy.wait_send()
-    for block, copy in near:
-        @pl.when(block < blocks)
-        def _(copy=copy):
-            copy.wait_send()
-    for block, copy in z_copies[1:]:
-        @pl.when(block < blocks)
-        def _(copy=copy):
-            copy.wait_send()
+        def _(u=u):
+            left(raw_row.at[pl.ds(0, 2)], raw_sem.at[0, u], twin)
+    left(raw_row, twin_sem.at[0], twin)
+    for p, (lo, hi) in enumerate(cuts):
+        left(rows_in.at[pl.ds(0, X * Y - 1), pl.ds(lo, hi - lo)], fwd_sem.at[0, p], twin)
+    twin0.wait_send()
+    twin1.wait_send()
+    left(back.at[pl.ds(0, X * Y - 1)], bwd_sem.at[0], twin)
+    left(outbox.at[pl.ds(0, 7)], near_sem.at[8], twin)
 
     @pl.when(has_block)
     def _():
-        for copy in ag:
-            copy.wait_send()
-    for from_block, relay in relays:
-        @pl.when(from_block < blocks)
-        def _(relay=relay):
-            relay.wait_send()
+        left(outbox.at[pl.ds(0, 6)], z_sem.at[4], twin)
+        left(emb_ref.at[:, pl.ds(0, 12 * LANE)], ag_sem.at[0], twin)
+
+    @pl.when(jnp.logical_not(has_block))
+    def _():
+        left(outbox.at[pl.ds(0, 7)], z_sem.at[4], twin)
+
+    full = (zl + 1) % 2 != c
+
+    @pl.when(full)
+    def _():
+        left(emb_ref.at[:, pl.ds(0, 16 * LANE)], rel_sem.at[4], twin)
+
+    @pl.when(jnp.logical_not(full))
+    def _():
+        left(emb_ref.at[:, pl.ds(0, 12 * LANE)], rel_sem.at[4], twin)
+
+
+def store(emb_ref, grad_ref, emb_out, grad_out, sem):
+    copies = [
+        pltpu.make_async_copy(grad_ref, grad_out, sem.at[0]),
+        pltpu.make_async_copy(emb_ref, emb_out, sem.at[1]),
+    ]
+    for copy in copies:
+        copy.start()
+    for copy in copies:
+        copy.wait()
 
 
 def body(token_ids, table, out_grad, groups, segs):
@@ -430,15 +424,17 @@
     vmem = pl.BlockSpec(memory_space=pltpu.VMEM)
     hbm = pl.BlockSpec(memory_space=pltpu.HBM)
     dma = pltpu.SemaphoreType.DMA
-    return pl.pallas_call(
+    shapes = (
+        jax.ShapeDtypeStruct((tok, depth), BF),
+        jax.ShapeDtypeStruct((lines, width), BF),
+    )
+    emb, grad = pl.pallas_call(
         kernel,
-        out_shape=(
-            jax.ShapeDtypeStruct((tok, depth), BF),
-            jax.ShapeDtypeStruct((lines, width), BF),
-        ),
-        in_specs=[vmem, hbm, hbm],
+        out_shape=shapes,
+        in_specs=[hbm, hbm, hbm],
         out_specs=(vmem, vmem),
         scratch_shapes=[
+            pltpu.VMEM((1, tok), jnp.int32),
             pltpu.VMEM((groups, 1, tok), jnp.int32),
             pltpu.VMEM((groups, cap, tok), jnp.int32),
             pltpu.VMEM((lines, width), BF),
@@ -458,23 +454,34 @@
             pltpu.VMEM((X * Y, 2, cap, width), BF),
             pltpu.VMEM((X * Y, 2, cap, width), BF),
             pltpu.VMEM((groups * cap, lines), BF),
+            dma((3,)),
             dma((2,)),
-            dma((2, groups)),
-            dma((2, Y)),
-            dma((2, 4)),
-            dma((2, 4)),
-            dma((2, X * Y, 2)),
+            dma((2,)),
             dma((2, 2)),
-            dma((2, 8)),
-            dma((2, 8)),
-            dma((2, X * Y)),
-            dma((2, Y, 4)),
-            dma((2, Y, 4)),
+            dma((2,)),
+            dma((2, 2)),
+            dma((2, 2)),
+            dma((9,)),
+            dma((5,)),
+            dma((2,)),
+            dma((4,)),
+            dma((5,)),
         ],
         compiler_params=pltpu.CompilerParams(
             collective_id=0, has_side_effects=True, vmem_limit_bytes=50 << 20
         ),
-    )(token_ids[None, :], table, out_grad.T)
+    )(*[
+        pltpu.with_memory_space_constraint(a, pltpu.HBM)
+        for a in (token_ids[None, :], table, out_grad.T)
+    ])
+    return pl.pallas_call(
+        store,
+        out_shape=shapes,
+        in_specs=[vmem, vmem],
+        out_specs=(hbm, hbm),
+        scratch_shapes=[dma((2,))],
+        compiler_params=pltpu.CompilerParams(vmem_limit_bytes=50 << 20),
+    )(emb, grad)
 
 
 def solution(mesh):

time: 70.7 us -> 66.1 us (0.935)
  local copies, waits for them, and re-layouts: 3.72 us -> 0 us
  Pallas kernels: 66.2 us -> 65.3 us
    unnamed x6 -> x0, local copies, waits for them, and re-layouts: 3.72 us -> none
    pallas_call x1 -> x2, Pallas kernels: 66.2 us -> 65.3 us  [the longest x1 63.6 us: body(): pl.pallas_call(kernel, out_shape=shapes, in_specs=[hbm, hbm, hbm], out_sp...]
where the time goes in v3:
time: 66.1 us; the launch traced here: 65.9 us
  Pallas kernels  65.3 us (99%)
    pallas_call x1, Pallas kernels, body(): pl.pallas_call(kernel, out_shape=shapes, in_specs=[hbm, hbm, hbm], out_sp...  63.6 us
    pallas_call x1, Pallas kernels, body(): pl.pallas_call(store, out_shape=shapes, in_specs=[vmem, vmem], out_specs=...  1.64 us

profile of v3, /device:TPU:1, one launch (start us, length us, event | category | flops | bytes accessed | tf_op | source)
XLA Modules:
  0.0 65.9 jit_solution(5380224673391244490)
XLA Ops:
  0.6 63.6 %shard_map.50 = (bf16[128,3584]{1,0:T(8,128)(2,1)S(1)}, bf16[1188,896]{1,0:T(8,128)(2,1)S(1)}) custom-call(s32[1,128]{1,0:T(1,128)} %bitcast.3, bf16[1188,896]{1,0:T(8,128)(2,1)} %table_ref.1, bf16[224,128]{1,0:T(8,128)(2,1)} %bitcast.2), custom_call_target="tpu_custom_call" | custom-call | tf_op jit(solution)/shard_map/pallas_call | solution.py:431
  64.3 1.6 %shard_map.51 = (bf16[128,3584]{1,0:T(8,128)(2,1)}, bf16[1188,896]{1,0:T(8,128)(2,1)}) custom-call(bf16[128,3584]{1,0:T(8,128)(2,1)S(1)} %get-tuple-element.4.emb_ref, bf16[1188,896]{1,0:T(8,128)(2,1)S(1)} %get-tuple-element.5.grad_ref), custom_call_target="tpu_custom_call" | custom-call | tf_op jit(solution)/shard_map/pallas_call | solution.py:477

commit v4 on v3

--- a/solution.py
+++ b/solution.py
@@ -235,8 +235,13 @@
     def block_of(d):
         return (along(d) - k + Z) % ZL
 
-    def within(block, p):
-        return (block >= cuts[p][0]) & (block < cuts[p][1])
+    ranks = [(0, 2), (2, Z)]
+
+    def within(block, p, plane, r):
+        return (
+            (block >= cuts[p][0]) & (block < cuts[p][1])
+            & (plane >= ranks[r][0]) & (plane < ranks[r][1])
+        )
 
     my_block = block_of(0)
     has_block = my_block < blocks
@@ -244,7 +249,7 @@
     near = []
     for n, (way, d) in enumerate(steps):
         block = block_of(d + (-4 if way else 4))
-        near.append((block, remote(
+        near.append((block, along(d + (-4 if way else 4)), remote(
             sums.at[jnp.minimum(block, blocks - 1)], inbox.at[n],
             near_sem.at[8], near_sem.at[n], at_z(-4 if way else 4),
         )))
@@ -255,25 +260,27 @@
         )))
     order = sorted(range(8), key=lambda n: -abs(steps[n][1]))
 
-    def send_z(p, copy):
+    def add_twin(p, copy):
         lo, hi = cuts[p]
         copy.wait_recv()
         for b in range(lo, hi):
             sums[b] = part[c, b] + halves[b]
+
+    def send_near(p, r):
         for n in order:
-            block, near_copy = near[n]
-
-            @pl.when(within(block, p))
+            block, plane, near_copy = near[n]
+
+            @pl.when(within(block, p, plane, r))
             def _(near_copy=near_copy):
                 near_copy.start()
 
-    def pass_z(p):
+    def pass_z(p, r):
         for n in order:
             block, z_copy = z_copies[n]
 
-            @pl.when(within(block, p))
+            @pl.when(within(block, p, along(steps[n][1]), r))
             def _(n=n, block=block, z_copy=z_copy):
-                near[n][1].wait_recv()
+                near[n][2].wait_recv()
                 both = sums[block] + inbox[n]
                 if steps[n][1] == 0:
                     zin[0, z % 4] = both
@@ -283,9 +290,12 @@
 
     twin0 = merge(0)
 
-    send_z(0, twin0)
+    add_twin(0, twin0)
+    send_near(0, 0)
     twin1 = merge(1)
-    send_z(1, twin1)
+    add_twin(1, twin1)
+    for p, r in [(1, 0), (0, 1), (1, 1)]:
+        send_near(p, r)
 
     for m in range(2):
         @pl.when(raw_from[m] != z)
@@ -311,9 +321,6 @@
         ).start()
     back[x * Y + pair] = back_out[mine]
 
-    pass_z(0)
-    pass_z(1)
-
     def columns(block, q):
         return pl.ds(pl.multiple_of(q * width + block * LANE, LANE), LANE)
 
@@ -333,14 +340,19 @@
                 out, sem.at[dy], peer,
             ))
 
-    @pl.when(has_block)
-    def _():
+    def gather():
         for d in range(4):
             arrived(outbox.at[pl.ds(0, 2 if d else 1)], z_sem.at[d], twin)
             cols = columns(my_block, quarter(d))
             emb_ref[:, cols] = zin[0, quarter(d)] + zin[1, quarter(d)]
             for dy in (2, 1, 3, 0):
                 ag[d * Y + dy].start()
+
+    pass_z(0, 0)
+    pass_z(1, 0)
+    pass_z(0, 1)
+    pass_z(1, 1)
+    pl.when(has_block)(gather)
 
     arrived(back.at[pl.ds(0, X * Y - 1)], bwd_sem.at[1], twin)
     out_ref[...] = lax.dot_general(

time: 66.1 us -> 65 us (0.983)
  Pallas kernels: 65.3 us -> 64.1 us
    pallas_call x1, Pallas kernels: 63.6 us -> 62.5 us  [body(): pl.pallas_call(kernel, out_shape=shapes, in_specs=[hbm, hbm, hbm], out_sp...]
where the time goes in v4:
time: 65 us; the launch traced here: 64.7 us
  Pallas kernels  64.1 us (99%)
    pallas_call x1, Pallas kernels, body(): pl.pallas_call(kernel, out_shape=shapes, in_specs=[hbm, hbm, hbm], out_sp...  62.5 us
    pallas_call x1, Pallas kernels, body(): pl.pallas_call(store, out_shape=shapes, in_specs=[vmem, vmem], out_specs=...  1.64 us

profile of v4, /device:TPU:1, one launch (start us, length us, event | category | flops | bytes accessed | tf_op | source)
XLA Modules:
  0.0 64.7 jit_solution(10440693349038486307)
XLA Ops:
  0.6 62.5 %shard_map.50 = (bf16[128,3584]{1,0:T(8,128)(2,1)S(1)}, bf16[1188,896]{1,0:T(8,128)(2,1)S(1)}) custom-call(s32[1,128]{1,0:T(1,128)} %bitcast.3, bf16[1188,896]{1,0:T(8,128)(2,1)} %table_ref.1, bf16[224,128]{1,0:T(8,128)(2,1)} %bitcast.2), custom_call_target="tpu_custom_call" | custom-call | tf_op jit(solution)/shard_map/pallas_call | solution.py:443
  63.1 1.6 %shard_map.51 = (bf16[128,3584]{1,0:T(8,128)(2,1)}, bf16[1188,896]{1,0:T(8,128)(2,1)}) custom-call(bf16[128,3584]{1,0:T(8,128)(2,1)S(1)} %get-tuple-element.4.emb_ref, bf16[1188,896]{1,0:T(8,128)(2,1)S(1)} %get-tuple-element.5.grad_ref), custom_call_target="tpu_custom_call" | custom-call | tf_op jit(solution)/shard_map/pallas_call | solution.py:489
